TPU v7x, 32 devices: a whole 2x2x4 slice. The times are simulated.
32 devices in a mesh: dp: 16 (over z, y, x), tensor: 2 (over core).
Axes of the slice: x: 2, y: 2, z: 4, core: 2. Of those that a mesh axis runs over, the one named last changes fastest.
Arguments:
- residual_in: float32 [16, 2048, 640], P('dp'), may hold values from -6 to 6
- cotangent: float32 [16, 2048, 640], P('dp'), may hold values from -6 to 6
- segment_ids: int32 [16, 2048], P('dp'), may hold values from 0 to 15, never falling along the last dimension, each value on 1 to 512 neighbouring positions
- gain_attn_in: float32 [640], replicated, may hold values from 0.25 to 1.75
- w_query: bfloat16 [640, 1024], P(None, 'tensor'), may hold values from -0.25 to 0.25
- w_key: bfloat16 [640, 256], replicated, may hold values from -0.25 to 0.25
- w_value: bfloat16 [640, 256], replicated, may hold values from -0.25 to 0.25
- gain_query: float32 [256], replicated, may hold values from 0.5 to 4
- gain_key: float32 [256], replicated, may hold values from 0.5 to 4
- w_out: bfloat16 [1024, 640], P('tensor'), may hold values from -0.1875 to 0.1875
- gain_attn_out: float32 [640], replicated, may hold values from 0.25 to 1.75
- gain_ff_in: float32 [640], replicated, may hold values from 0.25 to 1.75
- w_gate: bfloat16 [640, 2048], P(None, 'tensor'), may hold values from -0.25 to 0.25
- w_up: bfloat16 [640, 2048], P(None, 'tensor'), may hold values from -0.25 to 0.25
- w_down: bfloat16 [2048, 640], P('tensor'), may hold values from -0.125 to 0.125
- gain_ff_out: float32 [640], replicated, may hold values from 0.25 to 1.75
Outputs:
- output: float32 [16, 2048, 640], P('dp', 'tensor')
- grad_input: float32 [16, 2048, 640], P('dp', 'tensor')
- grad_gain_attn_in: float32 [640], replicated
- grad_w_query: float32 [640, 1024], P(None, ('tensor', 'dp'))
- grad_w_key: float32 [640, 256], replicated
- grad_w_value: float32 [640, 256], replicated
- grad_gain_query: float32 [256], replicated
- grad_gain_key: float32 [256], replicated
- grad_w_out: float32 [1024, 640], P('tensor', 'dp')
- grad_gain_attn_out: float32 [640], replicated
- grad_gain_ff_in: float32 [640], replicated
- grad_w_gate: float32 [640, 2048], P(None, ('tensor', 'dp'))
- grad_w_up: float32 [640, 2048], P(None, ('tensor', 'dp'))
- grad_w_down: float32 [2048, 640], P('tensor', 'dp')
- grad_gain_ff_out: float32 [640], replicated
Inputs may be any that keep to these rules, and one draw needn't show every extreme that they name: `segment_ids`: each row holds 16 sequences numbered from 0 upward in order without gaps; each has 1 to 512 tokens and some sequence of each row has exactly 512.
All inputs are finite; a program needn't handle non-finite values.
Results may differ from a plain program's by a relative error of at most 0.015.
The roundings to bfloat16 on the way count: a program that leaves them out, or rounds other values in their place, can miss the bound.
Values may be sent and summed in bfloat16 or wider, within the bound.
A program may use at most 256 MiB of HBM per device.

v0:
```python
import jax
import jax.numpy as jnp
from jax import lax
from jax.sharding import PartitionSpec as P

D = 640
HEAD_WIDTH = 256
BLOCK = 512
EPS = 1e-06
THETA = 1000000.0
SCORE_SCALE = 0.0625
GELU_C = 0.7978845608028654
GELU_A = 0.044715


def product(left, right):
    return jnp.dot(left, right, preferred_element_type=jnp.float32)


def product_tn(left, right):
    return lax.dot_general(
        left, right, (((0,), (0,)), ((), ())), preferred_element_type=jnp.float32
    )


def product_nt(left, right):
    return lax.dot_general(
        left, right, (((1,), (1,)), ((), ())), preferred_element_type=jnp.float32
    )


def rms_forward(values, gain):
    inv_rms = lax.rsqrt(jnp.mean(values * values, axis=-1, keepdims=True) + EPS)
    normed = values * inv_rms
    return (normed * gain, normed, inv_rms)


def rms_backward(normed, inv_rms, gain, upstream):
    scaled = upstream * gain
    return inv_rms * (scaled - normed * jnp.mean(scaled * normed, axis=-1, keepdims=True))


def positions_of(segment_row):
    token_count = segment_row.shape[0]
    index_row = jnp.arange(token_count, dtype=jnp.int32)
    first_pos = jnp.concatenate([jnp.ones((1,), bool), segment_row[1:] != segment_row[:-1]])
    start_row = lax.cummax(jnp.where(first_pos, index_row, 0), axis=0)
    return index_row - start_row


def rope_tables(positions):
    freq_index = jnp.arange(HEAD_WIDTH // 2, dtype=jnp.float32)
    inv_freq = jnp.exp(freq_index * (-2.0 * jnp.log(THETA) / HEAD_WIDTH))
    angles = positions.astype(jnp.float32)[:, None] * inv_freq[None, :]
    return (jnp.cos(angles)[:, None, :], jnp.sin(angles)[:, None, :])


def rotate(values, cos_tab, sin_tab, direction):
    half_a = values[..., : HEAD_WIDTH // 2]
    half_b = values[..., HEAD_WIDTH // 2 :]
    return jnp.concatenate(
        [
            half_a * cos_tab - direction * half_b * sin_tab,
            half_b * cos_tab + direction * half_a * sin_tab,
        ],
        axis=-1,
    )


def windows(values, front):
    blocks = values.shape[0] // BLOCK
    padded = jnp.concatenate([front, values], axis=0)
    padded = padded.reshape((blocks + 1, BLOCK) + values.shape[1:])
    return jnp.concatenate([padded[:-1], padded[1:]], axis=1)


def window_restore(win_grad):
    own_part = win_grad[:, BLOCK:]
    next_part = jnp.concatenate(
        [win_grad[1:, :BLOCK], jnp.zeros_like(win_grad[:1, :BLOCK])], axis=0
    )
    total = own_part + next_part
    return (total.reshape((total.shape[0] * BLOCK,) + total.shape[2:]), win_grad[0, :BLOCK])


def block_mask(segment_row):
    token_count = segment_row.shape[0]
    blocks = token_count // BLOCK
    index_row = jnp.arange(token_count, dtype=jnp.int32)
    filler = jnp.full((BLOCK,), -1, jnp.int32)
    key_seg = windows(segment_row, filler)
    key_index = windows(index_row, filler)
    query_seg = segment_row.reshape(blocks, BLOCK)
    query_index = index_row.reshape(blocks, BLOCK)
    return (key_seg[:, None, :] == query_seg[:, :, None]) & (
        key_index[:, None, :] <= query_index[:, :, None]
    )


def attn_scores(query_rot, key_rot, key_front, seg_mask):
    token_count, head_total_count = (query_rot.shape[0], query_rot.shape[1])
    blocks = token_count // BLOCK
    query_block = query_rot.reshape(blocks, BLOCK, head_total_count, HEAD_WIDTH)
    key_window = windows(key_rot, key_front)
    logit_scores = (
        jnp.einsum("pjlu,pvu->pljv", query_block, key_window, preferred_element_type=jnp.float32)
        * SCORE_SCALE
    )
    return (jnp.where(seg_mask[:, None], logit_scores, -jnp.inf), query_block, key_window)


def attend_forward(query_rot, key_rot, value_b, key_front, value_front, seg_mask):
    token_count, head_total_count = (query_rot.shape[0], query_rot.shape[1])
    logit_scores, query_block, key_window = attn_scores(query_rot, key_rot, key_front, seg_mask)
    value_window = windows(value_b, value_front)
    row_max = jnp.max(logit_scores, axis=-1, keepdims=True)
    log_total = row_max + jnp.log(jnp.sum(jnp.exp(logit_scores - row_max), axis=-1, keepdims=True))
    attention_weights = jnp.exp(logit_scores - log_total).astype(jnp.bfloat16)
    attention_mixed = jnp.einsum(
        "ipjv,ivx->ijpx", attention_weights, value_window, preferred_element_type=jnp.float32
    )
    return (attention_mixed.reshape(token_count, head_total_count, HEAD_WIDTH), log_total)


def attend_backward(
    query_rot,
    key_rot,
    value_b,
    key_front,
    value_front,
    seg_mask,
    attention_mixed,
    log_total,
    grad_out,
):
    token_count, head_total_count = (query_rot.shape[0], query_rot.shape[1])
    blocks = token_count // BLOCK
    logit_scores, query_block, key_window = attn_scores(query_rot, key_rot, key_front, seg_mask)
    value_window = windows(value_b, value_front)
    attention_weights = jnp.exp(logit_scores - log_total)
    probability_rows = attention_weights.astype(jnp.bfloat16)
    gradient_block = grad_out.reshape(blocks, BLOCK, head_total_count, HEAD_WIDTH)
    probability_gradient = jnp.einsum(
        "pjlu,pvu->pljv", gradient_block, value_window, preferred_element_type=jnp.float32
    )
    row_delta = jnp.sum(grad_out.astype(jnp.float32) * attention_mixed, axis=-1)
    row_delta = row_delta.reshape(blocks, BLOCK, head_total_count).transpose(0, 2, 1)[..., None]
    score_gradient = (attention_weights * (probability_gradient - row_delta) * SCORE_SCALE).astype(
        jnp.bfloat16
    )
    query_gradient = jnp.einsum(
        "ipjv,ivx->ijpx", score_gradient, key_window, preferred_element_type=jnp.float32
    )
    key_gradient, key_back = window_restore(
        jnp.einsum(
            "vptl,vtpm->vlm", score_gradient, query_block, preferred_element_type=jnp.float32
        )
    )
    value_gradient, value_back = window_restore(
        jnp.einsum(
            "vptl,vtpm->vlm", probability_rows, gradient_block, preferred_element_type=jnp.float32
        )
    )
    return (
        query_gradient.reshape(token_count, head_total_count, HEAD_WIDTH),
        key_gradient,
        value_gradient,
        key_back,
        value_back,
    )


def on_device(
    residual_in,
    cotangent,
    segment_ids,
    gain_attn_in,
    w_query,
    w_key,
    w_value,
    gain_query,
    gain_key,
    w_out,
    gain_attn_out,
    gain_ff_in,
    w_gate,
    w_up,
    w_down,
    gain_ff_out,
):
    inputs_all = residual_in[0]
    upstream_all = cotangent[0]
    segment_row = segment_ids[0]
    tok_total = inputs_all.shape[0]
    row_share = tok_total // lax.axis_size("tensor")
    first_row = lax.axis_index("tensor") * row_share

    def own_rows(values):
        return lax.dynamic_slice_in_dim(values, first_row, row_share, 0)

    def mine(values):
        return own_rows(values)

    cos_full, sin_full = rope_tables(positions_of(segment_row))
    mask_full = block_mask(segment_row)
    inputs, upstream, cos_tab, sin_tab, seg_mask = (
        inputs_all,
        upstream_all,
        cos_full,
        sin_full,
        mask_full,
    )
    query_full, gate_full, up_full, out_full, down_full = (w_query, w_gate, w_up, w_out, w_down)
    token_count = inputs.shape[0]
    head_total_count = query_full.shape[1] // HEAD_WIDTH
    normed_in, hat_in, inv_in = rms_forward(inputs, gain_attn_in)
    normed_b = normed_in.astype(jnp.bfloat16)
    query_lin = product(normed_b, query_full).reshape(token_count, head_total_count, HEAD_WIDTH)
    key_lin = product(normed_b, w_key).reshape(token_count, 1, HEAD_WIDTH)
    value_b = product(normed_b, w_value).astype(jnp.bfloat16)
    query_n, query_hat, query_inv = rms_forward(query_lin, gain_query)
    key_n, key_hat, key_inv = rms_forward(key_lin, gain_key)
    query_b = rotate(query_n, cos_tab, sin_tab, 1.0).astype(jnp.bfloat16)
    key_b = rotate(key_n, cos_tab, sin_tab, 1.0).astype(jnp.bfloat16)[:, 0]
    key_front = jnp.zeros((BLOCK, HEAD_WIDTH), jnp.bfloat16)
    value_front = jnp.zeros((BLOCK, HEAD_WIDTH), jnp.bfloat16)
    attention_mixed, log_total = attend_forward(
        query_b, key_b, value_b, key_front, value_front, seg_mask
    )
    attn_flat = attention_mixed.reshape(token_count, head_total_count * HEAD_WIDTH).astype(
        jnp.bfloat16
    )
    attn_part = product(attn_flat, out_full)
    attn_sum = lax.psum(attn_part, "tensor")
    branch_attn, hat_attn, inv_attn = rms_forward(attn_sum, gain_attn_out)
    middle = inputs + branch_attn
    normed_mid, hat_mid, inv_mid = rms_forward(middle, gain_ff_in)
    mid_b = normed_mid.astype(jnp.bfloat16)
    gate_proj = product(mid_b, gate_full)
    up_proj = product(mid_b, up_full)
    tanh_part = jnp.tanh(GELU_C * (gate_proj + GELU_A * gate_proj * gate_proj * gate_proj))
    gelu_val = 0.5 * gate_proj * (1.0 + tanh_part)
    act_b = (gelu_val * up_proj).astype(jnp.bfloat16)
    ff_part = product(act_b, down_full)
    ff_sum = lax.psum(ff_part, "tensor")
    branch_ff, hat_ff, inv_ff = rms_forward(ff_sum, gain_ff_out)
    output = middle + branch_ff
    query_width = query_full.shape[1] // w_query.shape[1]
    unit_width = gate_full.shape[1] // w_gate.shape[1]
    grad_gain_ff_out = jnp.sum(mine(upstream) * mine(hat_ff), axis=0)
    grad_ff = rms_backward(hat_ff, inv_ff, gain_ff_out, upstream).astype(jnp.bfloat16)
    grad_w_down = product_tn(act_b, grad_ff)
    grad_act = product_nt(grad_ff, down_full)
    gelu_deriv = 0.5 * (1.0 + tanh_part) + 0.5 * gate_proj * (
        1.0 - tanh_part * tanh_part
    ) * GELU_C * (1.0 + 3.0 * GELU_A * gate_proj * gate_proj)
    grad_gate = (grad_act * up_proj * gelu_deriv).astype(jnp.bfloat16)
    grad_up = (grad_act * gelu_val).astype(jnp.bfloat16)
    grad_w_gate = product_tn(mid_b, grad_gate).reshape(D, unit_width, -1)
    grad_w_up = product_tn(mid_b, grad_up).reshape(D, unit_width, -1)
    grad_w_down = grad_w_down.reshape(grad_w_down.shape[0], 1, D)
    grad_mid_n = product_nt(grad_gate, gate_full) + product_nt(grad_up, up_full)
    grad_gain_ff_in = jnp.sum(grad_mid_n * hat_mid, axis=0)
    mid_term = rms_backward(hat_mid, inv_mid, gain_ff_in, grad_mid_n)
    grad_middle = upstream + lax.psum(mid_term, "tensor")
    grad_gain_attn_out = jnp.sum(mine(grad_middle) * mine(hat_attn), axis=0)
    grad_attn_sum = rms_backward(hat_attn, inv_attn, gain_attn_out, grad_middle).astype(
        jnp.bfloat16
    )
    grad_w_out = product_tn(attn_flat, grad_attn_sum)
    grad_attn = (
        product_nt(grad_attn_sum, out_full)
        .astype(jnp.bfloat16)
        .reshape(token_count, head_total_count, HEAD_WIDTH)
    )
    key_backs = []
    value_backs = []
    query_gradient, key_gradient, value_gradient, key_back, value_back = attend_backward(
        query_b,
        key_b,
        value_b,
        key_front,
        value_front,
        seg_mask,
        attention_mixed,
        log_total,
        grad_attn,
    )
    key_backs.append(key_back)
    value_backs.append(value_back)
    grad_gain_key = jnp.zeros((HEAD_WIDTH,), jnp.float32)
    key_grad_n = rotate(key_gradient[:, None], cos_tab, sin_tab, -1.0)
    grad_gain_key = grad_gain_key + jnp.sum(key_grad_n * key_hat, axis=(0, 1))
    key_raw = rms_backward(key_hat, key_inv, gain_key, key_grad_n).astype(jnp.bfloat16)[:, 0]
    value_raw = value_gradient.astype(jnp.bfloat16)
    grad_w_key = product_tn(normed_b, key_raw)
    grad_w_value = product_tn(normed_b, value_raw)
    grad_normed = product_nt(key_raw, w_key) + product_nt(value_raw, w_value)
    query_grad_n = rotate(query_gradient, cos_tab, sin_tab, -1.0)
    grad_gain_query = jnp.sum(query_grad_n * query_hat, axis=(0, 1))
    query_raw = (
        rms_backward(query_hat, query_inv, gain_query, query_grad_n)
        .astype(jnp.bfloat16)
        .reshape(token_count, head_total_count * HEAD_WIDTH)
    )
    grad_w_query = product_tn(normed_b, query_raw).reshape(D, query_width, -1)
    grad_w_out = grad_w_out.reshape(grad_w_out.shape[0], 1, D)
    grad_normed = grad_normed + product_nt(query_raw, query_full)
    grad_gain_attn_in = jnp.sum(grad_normed * hat_in, axis=0)
    in_term = rms_backward(hat_in, inv_in, gain_attn_in, grad_normed)
    grad_input = grad_middle + lax.psum(in_term, "tensor")
    share_query, share_out, share_gate, share_up, share_down = (
        lax.psum_scatter(grad_w_query, "dp", scatter_dimension=2, tiled=True),
        lax.psum_scatter(grad_w_out, "dp", scatter_dimension=2, tiled=True),
        lax.psum_scatter(grad_w_gate, "dp", scatter_dimension=2, tiled=True),
        lax.psum_scatter(grad_w_up, "dp", scatter_dimension=2, tiled=True),
        lax.psum_scatter(grad_w_down, "dp", scatter_dimension=2, tiled=True),
    )
    share_query = share_query.reshape(D, -1)
    share_gate = share_gate.reshape(D, -1)
    share_up = share_up.reshape(D, -1)
    share_out = share_out.reshape(share_out.shape[0], -1)
    share_down = share_down.reshape(share_down.shape[0], -1)
    shared_sums = lax.psum(
        (
            grad_gain_attn_in,
            grad_w_key,
            grad_w_value,
            grad_gain_query,
            grad_gain_key,
            grad_gain_attn_out,
            grad_gain_ff_in,
            grad_gain_ff_out,
        ),
        ("dp", "tensor"),
    )
    return (
        mine(output)[None],
        mine(grad_input)[None],
        shared_sums[0],
        share_query,
        shared_sums[1],
        shared_sums[2],
        shared_sums[3],
        shared_sums[4],
        share_out,
        shared_sums[5],
        shared_sums[6],
        share_gate,
        share_up,
        share_down,
        shared_sums[7],
    )


def solution(mesh):
    return jax.shard_map(
        on_device,
        mesh=mesh,
        in_specs=(
            P("dp", None, None),
            P("dp", None, None),
            P("dp", None),
            P(),
            P(None, "tensor"),
            P(),
            P(),
            P(),
            P(),
            P("tensor", None),
            P(),
            P(),
            P(None, "tensor"),
            P(None, "tensor"),
            P("tensor", None),
            P(),
        ),
        out_specs=(
            P("dp", "tensor", None),
            P("dp", "tensor", None),
            P(),
            P(None, ("tensor", "dp")),
            P(),
            P(),
            P(),
            P(),
            P("tensor", "dp"),
            P(),
            P(),
            P(None, ("tensor", "dp")),
            P(None, ("tensor", "dp")),
            P("tensor", "dp"),
            P(),
        ),
        check_vma=False,
    )
```

profile of v0, /device:TPU:0, one launch (start us, length us, event | category | flops | bytes accessed | tf_op | source)
XLA Modules:
  0.0 851.9 jit_solution(15098856227065348030)
XLA Ops:
  18.8 6.0 broadcast_multiply_fusion.2
  25.1 5.5 fusion.44
  32.2 5.7 multiply_reduce_fusion.11
  50.3 5.0 fusion.4
  61.1 10.4 %bitcast_convert_fusion = (bf16[4,512,2,256]{1,3,2,0:T(8,128)(2,1)}, f32[4,256,2,512]{3,1,2,0:T(8,128)}) fusion(f32[4,1024,512,2]{2,1,3,0:T(8,128)} %copy-done.11, f32[4,2,512]{2,1,0:T(2,128)S(1)} %bitcast.255, pred[4,512,1024]{1,2,0:T(8,128)(4,1)S(1)} %compare_and_fusion, bf16[4,512,256]{1,2,0:T(8,128)(2,1)} %copy.69, bf16[4,512,256]{1,2,0:T(8,128)(2,1)} %copy.68), kind=kOutput, calls=%fused_computation.47 | convolution fusion | flops 2169503744 | bytes 27279360 | tf_op jit(solution)/shard_map/ipjv,ivx->ijpx/dot_general | solution.py:119
  71.5 5.4 copy.74
  82.9 32.5 %all-reduce.20.cloned.1.call-done = f32[2048,640]{1,0:T(8,128)} async-done(((f32[2048,640]{1,0:T(8,128)}), f32[2048,640]{1,0:T(8,128)}) %all-reduce.20.cloned.1.call-update) | async-done | bytes 5242896 | tf_op jit(solution)/shard_map/psum | solution.py:234
  130.6 7.2 multiply_convert_fusion.1
  139.7 5.1 fusion.62
  144.9 30.9 %all-reduce.22.cloned.1.call-done = f32[2048,640]{1,0:T(8,128)} async-done(((f32[2048,640]{1,0:T(8,128)}), f32[2048,640]{1,0:T(8,128)}) %all-reduce.22.cloned.1.call-update) | async-done | bytes 5242896 | tf_op jit(solution)/shard_map/psum | solution.py:245
  179.0 4.9 multiply_reduce_fusion.5
  186.5 15.7 %multiply_convert_fusion = (bf16[2048,1024]{1,0:T(8,128)(2,1)}, bf16[2048,1024]{1,0:T(8,128)(2,1)}) fusion(f32[2048,1024]{1,0:T(8,128)} %copy-done.71, f32[2048,1024]{1,0:T(8,128)} %get-tuple-element.99, bf16[2048,640]{1,0:T(8,128)(2,1)S(1)} %multiply_convert_fusion.3, bf16[1024,640]{1,0:T(8,128)(2,1)S(1)} %copy-done.66), kind=kOutput, calls=%fused_computation.18 | convolution fusion | flops 2732589056 | bytes 29097984 | tf_op jit(solution)/shard_map/dot_general | solution.py:27
  202.2 5.3 fusion.63
  207.5 6.1 multiply_reduce_fusion
  216.7 30.9 %all-reduce.24.cloned.1.call-done = f32[2048,640]{1,0:T(8,128)} async-done(((f32[2048,640]{1,0:T(8,128)}), f32[2048,640]{1,0:T(8,128)}) %all-reduce.24.cloned.1.call-update) | async-done | bytes 5242896 | tf_op jit(solution)/shard_map/psum | solution.py:265
  247.6 6.5 multiply_reduce_fusion.3
  270.8 12.1 %fusion.2 = bf16[4,2,512,1024]{2,3,1,0:T(8,128)(2,1)} fusion(f32[4,1024,512,2]{2,1,3,0:T(8,128)} %copy-done.11, bf16[4,512,2,256]{1,3,2,0:T(8,128)(2,1)S(1)} %copy.77, f32[4,2,512]{2,1,0:T(2,128)S(1)} %bitcast.254, f32[4,2,512]{2,1,0:T(2,128)S(1)} %bitcast.256, pred[4,512,1024]{1,2,0:T(8,128)(4,1)S(1)} %copy-done.16, ...), kind=kOutput, calls=%fused_computation.3 | convolution fusion | flops 2181038080 | bytes 31490048 | tf_op jit(solution)/shard_map/pjlu,pvu->pljv/dot_general | solution.py:143
  283.0 8.2 convolution_bitcast_fusion
  291.2 7.9 convolution_bitcast_fusion.2
  299.1 8.4 convolution_bitcast_fusion.1
  307.5 5.5 copy.81
  342.7 7.4 convolution_bitcast_fusion.5
  350.1 6.8 copy.85
  356.9 7.5 convolution_bitcast_fusion.4
  364.4 6.7 copy.86
  371.2 8.3 convolution_bitcast_fusion.3
  379.5 6.5 copy.87
  401.0 5.4 fusion.16
  410.0 5.3 multiply_reduce_fusion.12
  415.3 44.3 %all-reduce.10 = (f32[640]{0:T(1024)}, f32[256]{0:T(256)}, f32[256]{0:T(256)}, f32[640]{0:T(1024)}, f32[640]{0:T(1024)}, /*index=5*/f32[640]{0:T(1024)}) all-reduce(f32[640]{0:T(1024)S(1)} %get-tuple-element.47, f32[256]{0:T(256)S(1)} %get-tuple-element.49, ...), channel_id=1, replica_groups=mesh['dp'=16,'tensor'=2] {'dp','tensor'}, use_global_device_ids=true, to_apply=%region_22.23 | all-reduce | flops 3072 | bytes 24576 | tf_op jit(solution)/shard_map/psum | solution.py:324
  459.6 244.1 %all-reduce.30.cloned.1.call-done = (f32[640,1,512]{0,1,2:T(1,128)}, f32[512,1,640]{0,1,2:T(1,128)}, f32[640,1,1024]{0,1,2:T(1,128)}, f32[640,1,1024]{0,1,2:T(1,128)}, f32[1024,1,640]{0,1,2:T(1,128)}) async-done(((f32[640,1,512]{0,1,2:T(1,128)}, f32[512,1,640]{0,1,2:T(1,128)}, f32[640,1,1024]{0,1,2:T(1,128)}, f32[640,1,1024]{0,1,2:T(1,128)}, f32[1024,1,640]{0,1,2:T(1,128)}), (f32[640,1,512]{0,1,2:T(1,128)}, ...) | async-done | bytes 10485776
  711.7 129.2 %all-reduce.28.cloned.1.call-done = (f32[640,256]{1,0:T(8,128)}, f32[640,256]{1,0:T(8,128)}) async-done(((f32[640,256]{1,0:T(8,128)}, f32[640,256]{1,0:T(8,128)}), (f32[640,256]{1,0:T(8,128)}, f32[640,256]{1,0:T(8,128)})) %all-reduce.28.cloned.1.call-update) | async-done | bytes 1310736 | tf_op jit(solution)/shard_map/psum | solution.py:324
  (281 shorter events, 137.6 us)
Async XLA Ops:
  7.2 123.4 %copy-start = (bf16[640,1024]{1,0:T(8,128)(2,1)S(1)}, bf16[640,1024]{1,0:T(8,128)(2,1)}, u32[]{:S(2)}) copy-start(bf16[640,1024]{1,0:T(8,128)(2,1)} %param.29) | copy-start | bytes 3932164
  7.2 108.2 %all-reduce.20.cloned.1.call-start = ((), (), s32[]{:S(2)}) async-start(), calls=%async_computation | async-start | bytes 10485760 | tf_op jit(solution)/shard_map/psum | solution.py:234
  7.3 17.8 %copy-start.63 = (f32[128]{0:T(128)}, f32[128]{0:T(128)S(1)}, u32[]{:S(2)}) copy-start(f32[128]{0:T(128)S(1)} %multiply_exponential_fusion) | copy-start | bytes 1540
  14.8 23.1 %copy-start.44 = (f32[2048]{0:T(1024)}, f32[2048]{0:T(1024)S(1)}, u32[]{:S(2)}) copy-start(f32[2048]{0:T(1024)S(1)} %add_rsqrt_fusion.5) | copy-start | bytes 24580
  16.9 7.9 copy-start.60
  18.1 12.6 %copy-start.6 = (f32[2048,256]{1,0:T(8,128)}, f32[2048,256]{1,0:T(8,128)S(1)}, u32[]{:S(2)}) copy-start(f32[2048,256]{1,0:T(8,128)S(1)} %get-tuple-element.93) | copy-start | bytes 6291460
  18.1 12.6 %copy-start.48 = (f32[2048]{0:T(1024)}, f32[2048]{0:T(1024)S(1)}, u32[]{:S(2)}) copy-start(f32[2048]{0:T(1024)S(1)} %add_rsqrt_fusion.4) | copy-start | bytes 24580
  18.8 11.9 %copy-start.50 = (f32[2048]{0:T(1024)}, f32[2048]{0:T(1024)S(1)}, u32[]{:S(2)}) copy-start(f32[2048]{0:T(1024)S(1)} %fusion.52) | copy-start | bytes 24580
  38.0 8.9 %copy-start.46 = (f32[2048,2]{0,1:T(2,128)}, f32[2048,2]{0,1:T(2,128)S(1)}, u32[]{:S(2)}) copy-start(f32[2048,2]{0,1:T(2,128)S(1)} %add_rsqrt_fusion) | copy-start | bytes 49156
  44.5 16.6 %copy-start.15 = (pred[4,512,1024]{1,2,0:T(8,128)(4,1)}, pred[4,512,1024]{1,2,0:T(8,128)(4,1)S(1)}, u32[]{:S(2)}) copy-start(pred[4,512,1024]{1,2,0:T(8,128)(4,1)S(1)} %compare_and_fusion) | copy-start | bytes 6291460
  82.9 35.6 %copy-start.56 = (f32[640]{0:T(1024)S(1)}, f32[640]{0:T(1024)}, u32[]{:S(2)}) copy-start(f32[640]{0:T(1024)} %param.26) | copy-start | bytes 7684
  82.9 93.0 %all-reduce.22.cloned.1.call-start = ((), (), s32[]{:S(2)}) async-start(), calls=%async_computation.1 | async-start | bytes 10485760 | tf_op jit(solution)/shard_map/psum | solution.py:245
  130.6 9.2 %copy-start.65 = (bf16[1024,640]{1,0:T(8,128)(2,1)S(1)}, bf16[1024,640]{1,0:T(8,128)(2,1)}, u32[]{:S(2)}) copy-start(bf16[1024,640]{1,0:T(8,128)(2,1)} %param.30) | copy-start | bytes 3932164
  144.9 34.1 %copy-start.54 = (f32[640]{0:T(1024)S(1)}, f32[640]{0:T(1024)}, u32[]{:S(2)}) copy-start(f32[640]{0:T(1024)} %param.31) | copy-start | bytes 7684
  144.9 102.7 %all-reduce.24.cloned.1.call-start = ((), (), s32[]{:S(2)}) async-start(), calls=%async_computation.2 | async-start | bytes 10485760 | tf_op jit(solution)/shard_map/psum | solution.py:265
  175.9 8.0 slice-start.4
  183.9 23.6 %slice-start.6 = ((s8[5242880]{0:T(1024)(128)(4,1)}), s8[4194304]{0:T(1024)(128)(4,1)S(1)}, s32[]{:S(2)}) async-start(s8[5242880]{0:T(1024)(128)(4,1)} %bitcast.215), calls=%async_computation.12 | async-start | bytes 8388608
  186.5 15.7 %copy-start.28 = (bf16[2048,640]{1,0:T(8,128)(2,1)}, bf16[2048,640]{1,0:T(8,128)(2,1)S(1)}, u32[]{:S(2)}) copy-start(bf16[2048,640]{1,0:T(8,128)(2,1)S(1)} %multiply_convert_fusion.3) | copy-start | bytes 7864324
  186.5 15.7 %copy-start.68 = (bf16[640,1024]{1,0:T(8,128)(2,1)S(1)}, bf16[640,1024]{1,0:T(8,128)(2,1)}, u32[]{:S(2)}) copy-start(bf16[640,1024]{1,0:T(8,128)(2,1)} %param.28) | copy-start | bytes 3932164
  186.5 21.0 %slice-start.7 = ((s8[5242880]{0:T(1024)(128)(4,1)}), s8[1048576]{0:T(1024)(128)(4,1)S(1)}, s32[]{:S(2)}) async-start(s8[5242880]{0:T(1024)(128)(4,1)} %bitcast.215), calls=%async_computation.13 | async-start | bytes 2097152
  216.6 37.5 %slice-start.8 = ((s8[5242880]{0:T(1024)(128)(4,1)}), s8[1048576]{0:T(1024)(128)(4,1)S(1)}, s32[]{:S(2)}) async-start(s8[5242880]{0:T(1024)(128)(4,1)} %bitcast.217), calls=%async_computation.14 | async-start | bytes 2097152
  216.6 193.3 %all-reduce.26.cloned.1.call-start = ((), (), s32[]{:S(2)}) async-start(), calls=%async_computation.3 | async-start | bytes 10485760 | tf_op jit(solution)/shard_map/psum | solution.py:311
  266.6 16.3 %copy-start.17 = (bf16[4,512,2,256]{1,3,2,0:T(8,128)(2,1)}, bf16[4,512,2,256]{1,3,2,0:T(8,128)(2,1)S(1)}, u32[]{:S(2)}) copy-start(bf16[4,512,2,256]{1,3,2,0:T(8,128)(2,1)S(1)} %copy.77) | copy-start | bytes 6291460
  270.8 12.1 %copy-start.32 = (bf16[2048,1,128]{2,0,1:T(8,128)(2,1)S(1)}, bf16[2048,1,128]{2,0,1:T(8,128)(2,1)}, u32[]{:S(2)}) copy-start(bf16[2048,1,128]{2,0,1:T(8,128)(2,1)} %get-tuple-element.85) | copy-start | bytes 1572868
  270.8 12.1 %copy-start.33 = (bf16[2048,1,128]{2,0,1:T(8,128)(2,1)S(1)}, bf16[2048,1,128]{2,0,1:T(8,128)(2,1)}, u32[]{:S(2)}) copy-start(bf16[2048,1,128]{2,0,1:T(8,128)(2,1)} %get-tuple-element.86) | copy-start | bytes 1572868
  283.0 8.2 copy-start.40
  283.0 8.2 copy-start.41
  283.0 16.1 %slice-start.10 = ((s8[16777216]{0:T(1024)(128)(4,1)}), s8[4194304]{0:T(1024)(128)(4,1)S(1)}, s32[]{:S(2)}) async-start(s8[16777216]{0:T(1024)(128)(4,1)} %bitcast.219), calls=%async_computation.16 | async-start | bytes 8388608
  283.0 16.1 %slice-start.11 = ((s8[16777216]{0:T(1024)(128)(4,1)}), s8[4194304]{0:T(1024)(128)(4,1)S(1)}, s32[]{:S(2)}) async-start(s8[16777216]{0:T(1024)(128)(4,1)} %bitcast.219), calls=%async_computation.17 | async-start | bytes 8388608
  342.7 361.0 %all-reduce.30.cloned.1.call-start = ((), (), s32[]{:S(2)}) async-start(), calls=%async_computation.5 | async-start | bytes 20971520
  397.8 443.1 %all-reduce.28.cloned.1.call-start = ((), (), s32[]{:S(2)}) async-start(), calls=%async_computation.4 | async-start | bytes 2621440 | tf_op jit(solution)/shard_map/psum | solution.py:324
  410.0 434.9 %copy-start.1 = (bf16[640,1024]{1,0:T(8,128)(2,1)S(1)}, bf16[640,1024]{1,0:T(8,128)(2,1)}, u32[]{:S(2)}) copy-start(bf16[640,1024]{1,0:T(8,128)(2,1)} %param.29) | copy-start | bytes 3932164
  (60 other events, 224.8 us)
Sparse Core Ops, SparseCore 0:
  83.0 32.3 all-reduce.19
  145.0 30.8 all-reduce.21
  216.8 30.8 all-reduce.23
  342.8 30.8 all-reduce.25
  397.9 305.7 all-reduce.29
  709.7 131.2 all-reduce.27
where the time goes:
time: 856 us; the launch traced here: 852 us
  waiting for transfers between devices  468 us (55%)
  matrix products  148 us (17%)
  other arithmetic  90.9 us (11%)
  local copies, waits for them, and re-layouts  82.6 us (10%)
  blocking collectives  44.3 us (5%)
  between operations  17.4 us (2%)
    unnamed x7, waiting for transfers between devices  244 us
    psum x1, waiting for transfers between devices, on_device(): lax.psum((grad_gain_attn_in, grad_w_key, grad_w_value, grad_gain_query, g...  129 us
    psum x1, blocking collectives, on_device(): lax.psum((grad_gain_attn_in, grad_w_key, grad_w_value, grad_gain_query, g...  44.3 us
    dot_general x7, matrix products, product_nt(): lax.dot_general(left, right, (((1,), (1,)), ((), ())), preferred_element_...  34.4 us
    dot_general x7, matrix products, product_tn(): lax.dot_general(left, right, (((0,), (0,)), ((), ())), preferred_element_...  34.2 us
    psum x1, waiting for transfers between devices, on_device(): attn_sum = lax.psum(attn_part, 'tensor')  32.5 us
    unnamed x187, local copies, waits for them, and re-layouts  32.3 us
    psum x1, waiting for transfers between devices, on_device(): grad_middle = upstream + lax.psum(mid_term, 'tensor')  30.9 us
  transfers between devices with their start and end apart: 6, of which 5 were waited for; matrix products, arithmetic and copies ran while one was open for 9% of the time, Pallas kernels for 0%

commit v1 on v0

--- a/solution.py
+++ b/solution.py
@@ -322,17 +322,20 @@
     share_out = share_out.reshape(share_out.shape[0], -1)
     share_down = share_down.reshape(share_down.shape[0], -1)
     shared_sums = lax.psum(
-        (
-            grad_gain_attn_in,
-            grad_w_key,
-            grad_w_value,
-            grad_gain_query,
-            grad_gain_key,
-            grad_gain_attn_out,
-            grad_gain_ff_in,
-            grad_gain_ff_out,
+        lax.psum(
+            (
+                grad_gain_attn_in,
+                grad_w_key,
+                grad_w_value,
+                grad_gain_query,
+                grad_gain_key,
+                grad_gain_attn_out,
+                grad_gain_ff_in,
+                grad_gain_ff_out,
+            ),
+            "tensor",
         ),
-        ("dp", "tensor"),
+        "dp",
     )
     return (
         mine(output)[None],

time: 856 us -> 770 us (0.90)
  waiting for transfers between devices: 468 us -> 337 us
  blocking collectives: 44.3 us -> 85.5 us
    psum x1 -> x0, waiting for transfers between devices: 129 us -> none  [on_device(): lax.psum((grad_gain_attn_in, grad_w_key, grad_w_value, grad_gain_query, g...]
    psum x0 -> x1, blocking collectives: none -> 81.8 us  [on_device(): lax.psum(lax.psum((grad_gain_attn_in, grad_w_key, grad_w_value, grad_gain...]
    psum x1, blocking collectives: 44.3 us -> 3.74 us  [on_device(): lax.psum((grad_gain_attn_in, grad_w_key, grad_w_value, grad_gain_query, g...]
    unnamed x7 -> x6, waiting for transfers between devices: 244 us -> 243 us
  transfers between devices with their start and end apart: 6 -> 5, of which waited for: 5 -> 4; matrix products, arithmetic and copies ran while one was open for 9% -> 9% of each run, Pallas kernels for 0% -> 0%
where the time goes in v1:
time: 770 us; the launch traced here: 766 us
  waiting for transfers between devices  337 us (44%)
  matrix products  151 us (20%)
  other arithmetic  91.8 us (12%)
  blocking collectives  85.5 us (11%)
  local copies, waits for them, and re-layouts  83.1 us (11%)
  between operations  17.1 us (2%)
    unnamed x6, waiting for transfers between devices  243 us
    psum x1, blocking collectives, on_device(): lax.psum(lax.psum((grad_gain_attn_in, grad_w_key, grad_w_value, grad_gain...  81.8 us
    dot_general x7, matrix products, product_nt(): lax.dot_general(left, right, (((1,), (1,)), ((), ())), preferred_element_...  36.7 us
    dot_general x7, matrix products, product_tn(): lax.dot_general(left, right, (((0,), (0,)), ((), ())), preferred_element_...  34.9 us
    psum x1, waiting for transfers between devices, on_device(): attn_sum = lax.psum(attn_part, 'tensor')  32.5 us
    unnamed x187, local copies, waits for them, and re-layouts  31.6 us
    psum x1, waiting for transfers between devices, on_device(): grad_middle = upstream + lax.psum(mid_term, 'tensor')  30.9 us
    psum x1, waiting for transfers between devices, on_device(): ff_sum = lax.psum(ff_part, 'tensor')  30.9 us
  transfers between devices with their start and end apart: 5, of which 4 were waited for; matrix products, arithmetic and copies ran while one was open for 9% of the time, Pallas kernels for 0%

profile of v1, /device:TPU:0, one launch (start us, length us, event | category | flops | bytes accessed | tf_op | source)
XLA Modules:
  0.0 766.3 jit_solution(8173294327079431604)
XLA Ops:
  18.8 6.2 broadcast_multiply_fusion.2
  25.3 5.5 fusion.44
  32.3 5.7 multiply_reduce_fusion.11
  50.5 5.0 fusion.4
  61.3 10.4 %bitcast_convert_fusion = (bf16[4,512,2,256]{1,3,2,0:T(8,128)(2,1)}, f32[4,256,2,512]{3,1,2,0:T(8,128)}) fusion(f32[4,1024,512,2]{2,1,3,0:T(8,128)} %copy-done.11, f32[4,2,512]{2,1,0:T(2,128)S(1)} %bitcast.257, pred[4,512,1024]{1,2,0:T(8,128)(4,1)S(1)} %compare_and_fusion, bf16[4,512,256]{1,2,0:T(8,128)(2,1)} %copy.69, bf16[4,512,256]{1,2,0:T(8,128)(2,1)} %copy.68), kind=kOutput, calls=%fused_computation.47 | convolution fusion | flops 2169503744 | bytes 27279360 | tf_op jit(solution)/shard_map/ipjv,ivx->ijpx/dot_general | solution.py:119
  71.7 5.0 copy.74
  82.8 32.5 %all-reduce.20.cloned.1.call-done = f32[2048,640]{1,0:T(8,128)} async-done(((f32[2048,640]{1,0:T(8,128)}), f32[2048,640]{1,0:T(8,128)}) %all-reduce.20.cloned.1.call-update) | async-done | bytes 5242896 | tf_op jit(solution)/shard_map/psum | solution.py:234
  119.3 4.8 multiply_reduce_fusion.7
  130.4 7.2 multiply_convert_fusion.1
  139.6 5.1 fusion.62
  144.8 30.9 %all-reduce.22.cloned.1.call-done = f32[2048,640]{1,0:T(8,128)} async-done(((f32[2048,640]{1,0:T(8,128)}), f32[2048,640]{1,0:T(8,128)}) %all-reduce.22.cloned.1.call-update) | async-done | bytes 5242896 | tf_op jit(solution)/shard_map/psum | solution.py:245
  178.8 4.9 multiply_reduce_fusion.5
  186.4 15.7 %multiply_convert_fusion = (bf16[2048,1024]{1,0:T(8,128)(2,1)}, bf16[2048,1024]{1,0:T(8,128)(2,1)}) fusion(f32[2048,1024]{1,0:T(8,128)} %copy-done.69, f32[2048,1024]{1,0:T(8,128)} %get-tuple-element.108, bf16[2048,640]{1,0:T(8,128)(2,1)S(1)} %multiply_convert_fusion.3, bf16[1024,640]{1,0:T(8,128)(2,1)S(1)} %copy-done.64), kind=kOutput, calls=%fused_computation.18 | convolution fusion | flops 2732589056 | bytes 29097984 | tf_op jit(solution)/shard_map/dot_general | solution.py:27
  202.1 5.3 fusion.63
  207.4 6.1 multiply_reduce_fusion
  216.5 30.9 %all-reduce.24.cloned.1.call-done = f32[2048,640]{1,0:T(8,128)} async-done(((f32[2048,640]{1,0:T(8,128)}), f32[2048,640]{1,0:T(8,128)}) %all-reduce.24.cloned.1.call-update) | async-done | bytes 5242896 | tf_op jit(solution)/shard_map/psum | solution.py:265
  247.5 6.5 multiply_reduce_fusion.3
  261.8 4.7 copy.77
  270.7 12.1 %fusion.2 = bf16[4,2,512,1024]{2,3,1,0:T(8,128)(2,1)} fusion(f32[4,1024,512,2]{2,1,3,0:T(8,128)} %copy-done.11, bf16[4,512,2,256]{1,3,2,0:T(8,128)(2,1)S(1)} %copy.77, f32[4,2,512]{2,1,0:T(2,128)S(1)} %bitcast.256, f32[4,2,512]{2,1,0:T(2,128)S(1)} %bitcast.258, pred[4,512,1024]{1,2,0:T(8,128)(4,1)S(1)} %copy-done.16, ...), kind=kOutput, calls=%fused_computation.3 | convolution fusion | flops 2181038080 | bytes 31490048 | tf_op jit(solution)/shard_map/pjlu,pvu->pljv/dot_general | solution.py:143
  282.9 8.2 %convolution_bitcast_fusion = f32[4,512,2,256]{1,3,2,0:T(8,128)} fusion(bf16[4,2,512,1024]{2,3,1,0:T(8,128)(2,1)} %fusion.2, bf16[4,512,128]{2,1,0:T(8,128)(2,1)S(1)} %bitcast.240, bf16[4,512,128]{2,1,0:T(8,128)(2,1)S(1)} %bitcast.237, bf16[4,512,256]{2,1,0:T(8,128)(2,1)} %bitcast.242), kind=kOutput, calls=%fused_computation.74 | convolution fusion | flops 2153775104 | bytes 14680064 | tf_op jit(solution)/shard_map/ipjv,ivx->ijpx/dot_general | solution.py:151
  291.1 7.9 %convolution_bitcast_fusion.2 = f32[4,1024,256]{2,1,0:T(8,128)} fusion(bf16[4,2,512,1024]{2,3,1,0:T(8,128)(2,1)} %fusion.2, bf16[4,512,2,128]{3,1,0,2:T(8,128)(2,1)S(1)} %bitcast.246, bf16[4,512,2,128]{3,1,0,2:T(8,128)(2,1)S(1)} %bitcast.244), kind=kOutput, calls=%fused_computation.76 | convolution fusion | flops 2151677952 | bytes 14680064 | tf_op jit(solution)/shard_map/vptl,vtpm->vlm/dot_general | solution.py:155
  299.0 8.3 %convolution_bitcast_fusion.1 = f32[4,1024,256]{2,1,0:T(8,128)} fusion(bf16[4,512,2,256]{1,3,2,0:T(8,128)(2,1)} %copy-done.17, f32[4,1024,512,2]{2,1,3,0:T(8,128)S(1)} %bitcast.222, f32[4,2,512]{2,1,0:T(2,128)S(1)} %bitcast.259, pred[4,512,1024]{1,2,0:T(8,128)(4,1)} %copy-done.15), kind=kOutput, calls=%fused_computation.75 | convolution fusion | flops 2164260864 | bytes 25182208 | tf_op jit(solution)/shard_map/vptl,vtpm->vlm/dot_general | solution.py:160
  322.2 5.4 copy.81
  350.6 7.4 convolution_bitcast_fusion.5
  358.0 6.9 copy.85
  364.9 7.5 convolution_bitcast_fusion.4
  372.4 6.6 copy.86
  379.1 9.1 %convolution_bitcast_fusion.3 = f32[1024,1,640]{2,0,1:T(8,128)} fusion(bf16[2048,1024]{1,0:T(8,128)(2,1)} %copy-done.68, bf16[2048,640]{1,0:T(8,128)(2,1)} %copy-done.24), kind=kOutput, calls=%fused_computation.99 | convolution fusion | flops 2684354560 | bytes 9437184 | tf_op jit(solution)/shard_map/dot_general | solution.py:21
  388.2 6.5 copy.87
  409.7 5.3 fusion.16
  424.2 81.8 %all-reduce.10 = (f32[640]{0:T(1024)}, f32[256]{0:T(256)}, f32[256]{0:T(256)}, f32[640]{0:T(1024)}, f32[640]{0:T(1024)}, /*index=5*/f32[640]{0:T(1024)}) all-reduce(f32[640]{0:T(1024)S(1)} %get-tuple-element.66, f32[256]{0:T(256)S(1)} %get-tuple-element.67, ...), channel_id=1, replica_groups=mesh['dp'=16,'tensor'=2] {'dp'}, use_global_device_ids=true, to_apply=%region_23.24 | all-reduce | flops 3072 | bytes 24576 | tf_op jit(solution)/shard_map/psum | solution.py:324
  506.0 242.7 %all-reduce.26.cloned.1.call-done = (f32[640,1,512]{0,1,2:T(1,128)}, f32[640,256]{1,0:T(8,128)}, f32[640,256]{1,0:T(8,128)}, f32[512,1,640]{0,1,2:T(1,128)}, f32...) async-done(((f32[640,1,512]{0,1,2:T(1,128)}, f32[640,256]{1,0:T(8,128)}, f32[640,256]{1,0:T(8,128)}, f32[512,1,640]{0,1,2:T(1,128)}, ...) | async-done | bytes 11796496
  (280 shorter events, 141.0 us)
Async XLA Ops:
  7.2 123.2 %copy-start = (bf16[640,1024]{1,0:T(8,128)(2,1)S(1)}, bf16[640,1024]{1,0:T(8,128)(2,1)}, u32[]{:S(2)}) copy-start(bf16[640,1024]{1,0:T(8,128)(2,1)} %param.29) | copy-start | bytes 3932164
  7.2 108.0 %all-reduce.20.cloned.1.call-start = ((), (), s32[]{:S(2)}) async-start(), calls=%async_computation | async-start | bytes 10485760 | tf_op jit(solution)/shard_map/psum | solution.py:234
  7.3 18.0 %copy-start.61 = (f32[128]{0:T(128)}, f32[128]{0:T(128)S(1)}, u32[]{:S(2)}) copy-start(f32[128]{0:T(128)S(1)} %multiply_exponential_fusion) | copy-start | bytes 1540
  14.8 23.3 %copy-start.42 = (f32[2048]{0:T(1024)}, f32[2048]{0:T(1024)S(1)}, u32[]{:S(2)}) copy-start(f32[2048]{0:T(1024)S(1)} %add_rsqrt_fusion.5) | copy-start | bytes 24580
  16.9 8.1 %copy-start.56 = (f32[256]{0:T(256)S(1)}, f32[256]{0:T(256)}, u32[]{:S(2)}) copy-start(f32[256]{0:T(256)} %param.24) | copy-start | bytes 3076
  18.1 12.8 %copy-start.6 = (f32[2048,256]{1,0:T(8,128)}, f32[2048,256]{1,0:T(8,128)S(1)}, u32[]{:S(2)}) copy-start(f32[2048,256]{1,0:T(8,128)S(1)} %get-tuple-element.102) | copy-start | bytes 6291460
  18.1 12.7 %copy-start.46 = (f32[2048]{0:T(1024)}, f32[2048]{0:T(1024)S(1)}, u32[]{:S(2)}) copy-start(f32[2048]{0:T(1024)S(1)} %add_rsqrt_fusion.4) | copy-start | bytes 24580
  18.8 12.1 %copy-start.48 = (f32[2048]{0:T(1024)}, f32[2048]{0:T(1024)S(1)}, u32[]{:S(2)}) copy-start(f32[2048]{0:T(1024)S(1)} %fusion.52) | copy-start | bytes 24580
  38.2 8.9 %copy-start.44 = (f32[2048,2]{0,1:T(2,128)}, f32[2048,2]{0,1:T(2,128)S(1)}, u32[]{:S(2)}) copy-start(f32[2048,2]{0,1:T(2,128)S(1)} %add_rsqrt_fusion) | copy-start | bytes 49156
  44.6 16.6 %copy-start.15 = (pred[4,512,1024]{1,2,0:T(8,128)(4,1)}, pred[4,512,1024]{1,2,0:T(8,128)(4,1)S(1)}, u32[]{:S(2)}) copy-start(pred[4,512,1024]{1,2,0:T(8,128)(4,1)S(1)} %compare_and_fusion) | copy-start | bytes 6291460
  82.7 35.6 %copy-start.54 = (f32[640]{0:T(1024)S(1)}, f32[640]{0:T(1024)}, u32[]{:S(2)}) copy-start(f32[640]{0:T(1024)} %param.26) | copy-start | bytes 7684
  82.7 93.0 %all-reduce.22.cloned.1.call-start = ((), (), s32[]{:S(2)}) async-start(), calls=%async_computation.1 | async-start | bytes 10485760 | tf_op jit(solution)/shard_map/psum | solution.py:245
  130.4 9.2 %copy-start.63 = (bf16[1024,640]{1,0:T(8,128)(2,1)S(1)}, bf16[1024,640]{1,0:T(8,128)(2,1)}, u32[]{:S(2)}) copy-start(bf16[1024,640]{1,0:T(8,128)(2,1)} %param.30) | copy-start | bytes 3932164
  144.7 34.1 %copy-start.52 = (f32[640]{0:T(1024)S(1)}, f32[640]{0:T(1024)}, u32[]{:S(2)}) copy-start(f32[640]{0:T(1024)} %param.31) | copy-start | bytes 7684
  144.7 102.8 %all-reduce.24.cloned.1.call-start = ((), (), s32[]{:S(2)}) async-start(), calls=%async_computation.2 | async-start | bytes 10485760 | tf_op jit(solution)/shard_map/psum | solution.py:265
  175.7 8.1 %slice-start.4 = ((s8[5242880]{0:T(1024)(128)(4,1)}), s8[4194304]{0:T(1024)(128)(4,1)S(1)}, s32[]{:S(2)}) async-start(s8[5242880]{0:T(1024)(128)(4,1)} %bitcast.213), calls=%async_computation.9 | async-start | bytes 8388608
  183.8 23.6 %slice-start.6 = ((s8[5242880]{0:T(1024)(128)(4,1)}), s8[4194304]{0:T(1024)(128)(4,1)S(1)}, s32[]{:S(2)}) async-start(s8[5242880]{0:T(1024)(128)(4,1)} %bitcast.215), calls=%async_computation.11 | async-start | bytes 8388608
  186.4 15.7 %copy-start.24 = (bf16[2048,640]{1,0:T(8,128)(2,1)}, bf16[2048,640]{1,0:T(8,128)(2,1)S(1)}, u32[]{:S(2)}) copy-start(bf16[2048,640]{1,0:T(8,128)(2,1)S(1)} %multiply_convert_fusion.3) | copy-start | bytes 7864324
  186.4 15.7 %copy-start.66 = (bf16[640,1024]{1,0:T(8,128)(2,1)S(1)}, bf16[640,1024]{1,0:T(8,128)(2,1)}, u32[]{:S(2)}) copy-start(bf16[640,1024]{1,0:T(8,128)(2,1)} %param.28) | copy-start | bytes 3932164
  186.4 21.0 %slice-start.7 = ((s8[5242880]{0:T(1024)(128)(4,1)}), s8[1048576]{0:T(1024)(128)(4,1)S(1)}, s32[]{:S(2)}) async-start(s8[5242880]{0:T(1024)(128)(4,1)} %bitcast.215), calls=%async_computation.12 | async-start | bytes 2097152
  216.5 37.5 %slice-start.8 = ((s8[5242880]{0:T(1024)(128)(4,1)}), s8[1048576]{0:T(1024)(128)(4,1)S(1)}, s32[]{:S(2)}) async-start(s8[5242880]{0:T(1024)(128)(4,1)} %bitcast.217), calls=%async_computation.13 | async-start | bytes 2097152
  216.5 190.0 %all-reduce.28.cloned.1.call-start = ((), (), s32[]{:S(2)}) async-start(), calls=%async_computation.4 | async-start | bytes 13107200 | tf_op jit(solution)/shard_map/psum | solution.py:311
  266.5 16.3 %copy-start.17 = (bf16[4,512,2,256]{1,3,2,0:T(8,128)(2,1)}, bf16[4,512,2,256]{1,3,2,0:T(8,128)(2,1)S(1)}, u32[]{:S(2)}) copy-start(bf16[4,512,2,256]{1,3,2,0:T(8,128)(2,1)S(1)} %copy.77) | copy-start | bytes 6291460
  270.7 12.1 %copy-start.28 = (bf16[2048,1,128]{2,0,1:T(8,128)(2,1)S(1)}, bf16[2048,1,128]{2,0,1:T(8,128)(2,1)}, u32[]{:S(2)}) copy-start(bf16[2048,1,128]{2,0,1:T(8,128)(2,1)} %get-tuple-element.94) | copy-start | bytes 1572868
  270.7 12.1 %copy-start.29 = (bf16[2048,1,128]{2,0,1:T(8,128)(2,1)S(1)}, bf16[2048,1,128]{2,0,1:T(8,128)(2,1)}, u32[]{:S(2)}) copy-start(bf16[2048,1,128]{2,0,1:T(8,128)(2,1)} %get-tuple-element.95) | copy-start | bytes 1572868
  282.8 8.2 %copy-start.37 = (bf16[2048,2,128]{2,0,1:T(8,128)(2,1)S(1)}, bf16[2048,2,128]{2,0,1:T(8,128)(2,1)}, u32[]{:S(2)}) copy-start(bf16[2048,2,128]{2,0,1:T(8,128)(2,1)} %get-tuple-element.86) | copy-start | bytes 3145732
  282.8 8.2 %copy-start.38 = (bf16[2048,2,128]{2,0,1:T(8,128)(2,1)S(1)}, bf16[2048,2,128]{2,0,1:T(8,128)(2,1)}, u32[]{:S(2)}) copy-start(bf16[2048,2,128]{2,0,1:T(8,128)(2,1)} %get-tuple-element.87) | copy-start | bytes 3145732
  282.8 16.1 %slice-start.12 = ((s8[16777216]{0:T(1024)(128)(4,1)}), s8[4194304]{0:T(1024)(128)(4,1)S(1)}, s32[]{:S(2)}) async-start(s8[16777216]{0:T(1024)(128)(4,1)} %bitcast.221), calls=%async_computation.17 | async-start | bytes 8388608
  282.8 16.1 %slice-start.13 = ((s8[16777216]{0:T(1024)(128)(4,1)}), s8[4194304]{0:T(1024)(128)(4,1)S(1)}, s32[]{:S(2)}) async-start(s8[16777216]{0:T(1024)(128)(4,1)} %bitcast.221), calls=%async_computation.18 | async-start | bytes 8388608
  350.6 398.1 %all-reduce.26.cloned.1.call-start = ((), (), s32[]{:S(2)}) async-start(), calls=%async_computation.3 | async-start | bytes 23592960
  415.8 343.7 %copy-start.1 = (bf16[640,1024]{1,0:T(8,128)(2,1)S(1)}, bf16[640,1024]{1,0:T(8,128)(2,1)}, u32[]{:S(2)}) copy-start(bf16[640,1024]{1,0:T(8,128)(2,1)} %param.29) | copy-start | bytes 3932164
  748.6 10.0 %copy-start.41 = (f32[640,256]{1,0:T(8,128)S(1)}, f32[640,256]{1,0:T(8,128)}, u32[]{:S(2)}) copy-start(f32[640,256]{1,0:T(8,128)} %get-tuple-element.118) | copy-start | bytes 1966084
  (59 other events, 243.7 us)
Sparse Core Ops, SparseCore 0:
  82.8 32.3 all-reduce.19
  144.8 30.8 all-reduce.21
  216.6 30.8 all-reduce.23
  350.7 34.2 all-reduce.27
  406.6 341.9 all-reduce.25
